TPU v7x, 512 devices: a whole 4x8x8 slice. The times are simulated.
512 devices in a mesh: sx: 32 (over z_hi, x, core), sy: 16 (over z_lo, y).
Axes of the slice: x: 4, y: 8, z: 8 (z_hi: 4, z_lo: 2; z = z_hi * 2 + z_lo), core: 2. Of those that a mesh axis runs over, the one named last changes fastest.
Arguments:
- sources: bfloat16 [32, 16, 2, 64, 4096], P('sx', 'sy'), may hold values from -6 to 6
- translate_re: bfloat16 [4, 2, 2, 64, 64], replicated, may hold values from -0.375 to 0.375
- translate_im: bfloat16 [4, 2, 2, 64, 64], replicated, may hold values from -0.375 to 0.375
- frame_index: int32 [32, 16, 16], P('sx', 'sy'), may hold values from 0 to 4095
- velocity_index: int32 [32, 16, 256], P('sx', 'sy'), may hold values from 0 to 4095
- eval_re: bfloat16 [64, 64], replicated, may hold values from -1.5 to 1.5
- eval_im: bfloat16 [64, 64], replicated, may hold values from -1.5 to 1.5
- window: int32 [32, 16], P('sx', 'sy'), may hold values from 1 to 2
Outputs:
- smoothed: bfloat16 [256, 128, 4096], P('sx', 'sy')
All inputs are finite; a program needn't handle non-finite values.
Results may differ from a plain program's by a relative error of at most 0.0076.
Values may be sent and summed in bfloat16 or wider, within the bound.
No kernel may reach another device: no remote copies, remote signals or barrier semaphores. Data moves between devices by JAX's collectives and lax.ppermute only.
A program may use at most 64 MiB of HBM per device.

v0:
```python
import math

import jax
import jax.numpy as jnp
from jax import lax
from jax.sharding import PartitionSpec as P

LEVELS = 4
VGRID = 4096


TWO_PI = 2.0 * math.pi


def swapped(block, axis, bit):
    count = lax.axis_size(axis)
    route = []
    for low in range(count):
        high = low | 1 << bit
        if high != low and high < count:
            route += [(low, high), (high, low)]
    return lax.ppermute(block, axis, route)


def with_halo(block, sides, width):
    for axis, dim in sides:
        count = lax.axis_size(axis)
        forward = [(i, i + 1) for i in range(count - 1)]
        backward = [(target, source) for source, target in forward]
        low = lax.ppermute(
            lax.slice_in_dim(block, block.shape[dim] - width, None, axis=dim), axis, forward
        )
        high = lax.ppermute(lax.slice_in_dim(block, 0, width, axis=dim), axis, backward)
        block = jnp.concatenate([low, block, high], axis=dim)
    return block


def blocks(real_part, imag_part):
    upper = jnp.concatenate([real_part, -imag_part], axis=-1)
    lower = jnp.concatenate([imag_part, real_part], axis=-1)
    return jnp.concatenate([upper, lower], axis=-2)


def on_device(
    sources, translate_re, translate_im, frame_index, velocity_index, eval_re, eval_im, window
):
    terms = sources.shape[3]
    columns = sources.shape[4]
    state_flat = sources[0, 0].reshape(2 * terms, columns)
    base_product = frame_index[0, 0][:, None] * velocity_index[0, 0][None, :]
    for level_no in range(LEVELS):
        if level_no % 2 == 0:
            bit_pos = lax.axis_size("sx").bit_length() - 2 - level_no // 2
            own_bit = lax.axis_index("sx") >> bit_pos & 1
        else:
            bit_pos = lax.axis_size("sy").bit_length() - 2 - level_no // 2
            own_bit = lax.axis_index("sy") >> bit_pos & 1
        self_matrix = blocks(translate_re[level_no, own_bit, 0], translate_im[level_no, own_bit, 0])
        own_part = jnp.dot(self_matrix, state_flat, preferred_element_type=jnp.float32)
        if level_no % 2 == 0:
            received = swapped(state_flat, "sx", bit_pos)
        else:
            received = swapped(state_flat, "sy", bit_pos)
        other_matrix = blocks(
            translate_re[level_no, own_bit, 1], translate_im[level_no, own_bit, 1]
        )
        total = own_part + jnp.dot(other_matrix, received, preferred_element_type=jnp.float32)
        product = base_product * (level_no + 1) % VGRID
        angles = (TWO_PI / VGRID * product.astype(jnp.float32)).reshape(columns)
        cosine = jnp.cos(angles)[None, :]
        sine_part = jnp.sin(angles)[None, :]
        real_total = total[:terms]
        imag_total = total[terms:]
        new_real = cosine * real_total - sine_part * imag_total
        new_imag = sine_part * real_total + cosine * imag_total
        state_flat = jnp.concatenate([new_real, new_imag], axis=0).astype(jnp.bfloat16)
    evaluate = jnp.concatenate([eval_re, -eval_im], axis=1)
    side = math.isqrt(eval_re.shape[0])
    picture = jnp.dot(evaluate, state_flat, preferred_element_type=jnp.float32).astype(jnp.bfloat16)
    picture = picture.reshape(side, side, columns)
    padded = with_halo(picture, (("sx", 0), ("sy", 1)), 2)
    values = padded.astype(jnp.float32)
    rows_near = values[1:-3] + values[2:-2] + values[3:-1]
    rows_far = rows_near + values[0:-4] + values[4:]
    box_near = rows_near[:, 1:-3] + rows_near[:, 2:-2] + rows_near[:, 3:-1]
    box_far = (
        rows_far[:, 1:-3]
        + rows_far[:, 2:-2]
        + rows_far[:, 3:-1]
        + rows_far[:, 0:-4]
        + rows_far[:, 4:]
    )
    chosen = jnp.where(window[0, 0] == 2, box_far / 25.0, box_near / 9.0)
    return chosen.astype(jnp.bfloat16)


def solution(mesh):
    return jax.shard_map(
        on_device,
        mesh=mesh,
        in_specs=(
            P("sx", "sy", None, None, None),
            P(),
            P(),
            P("sx", "sy", None),
            P("sx", "sy", None),
            P(),
            P(),
            P("sx", "sy"),
        ),
        out_specs=P("sx", "sy", None),
        check_vma=False,
    )
```

profile of v0, /device:TPU:159, one launch (start us, length us, event | category | flops | bytes accessed | tf_op | source)
XLA Modules:
  0.0 221.6 jit_solution(4073111978079161416)
XLA Ops:
  0.0 8.8 %collective-permute-start = (bf16[128,4096]{1,0:T(8,128)(2,1)}, bf16[128,4096]{1,0:T(8,128)(2,1)S(1)}, u32[]{:S(2)}, u32[]{:S(2)}) collective-permute-start(bf16[128,4096]{1,0:T(8,128)(2,1)} %bitcast.58), channel_id=1, source_target_pairs={{0,256},{256,0},{16,272},{272,16},{32,288},{288,32},{48,304},{304,... | collective-permute-start | bytes 3145736 | tf_op jit(solution)/shard_map/ppermute | solution.py:22
  8.8 0.8 multiply_bitcast_fusion
  9.6 0.9 dynamic-slice_bitcast_fusion.1
  10.5 0.9 fusion.99
  11.6 1.7 fusion.31
  13.4 41.8 %collective-permute-done = bf16[128,4096]{1,0:T(8,128)(2,1)S(1)} collective-permute-done((bf16[128,4096]{1,0:T(8,128)(2,1)}, bf16[128,4096]{1,0:T(8,128)(2,1)S(1)}, u32[]{:S(2)}, u32[]{:S(2)}) %collective-permute-start) | collective-permute-done | bytes 1048608 | tf_op jit(solution)/shard_map/ppermute | solution.py:22
  55.1 0.5 convolution_add_fusion.3
  56.0 1.9 collective-permute-start.1
  57.9 0.5 fusion.23
  58.4 23.6 %collective-permute-done.1 = bf16[128,4096]{1,0:T(8,128)(2,1)S(1)} collective-permute-done((bf16[128,4096]{1,0:T(8,128)(2,1)S(1)}, bf16[128,4096]{1,0:T(8,128)(2,1)S(1)}, u32[]{:S(2)}, u32[]{:S(2)}) %collective-permute-start.1) | collective-permute-done | bytes 1048608 | tf_op jit(solution)/shard_map/ppermute | solution.py:22
  82.0 0.5 convolution_add_fusion.2
  82.9 1.9 collective-permute-start.2
  84.8 0.5 fusion.15
  85.3 44.8 %collective-permute-done.2 = bf16[128,4096]{1,0:T(8,128)(2,1)S(1)} collective-permute-done((bf16[128,4096]{1,0:T(8,128)(2,1)S(1)}, bf16[128,4096]{1,0:T(8,128)(2,1)S(1)}, u32[]{:S(2)}, u32[]{:S(2)}) %collective-permute-start.2) | collective-permute-done | bytes 1048608 | tf_op jit(solution)/shard_map/ppermute | solution.py:22
  130.1 0.5 convolution_add_fusion.1
  131.0 4.8 %collective-permute-start.3 = (bf16[128,4096]{1,0:T(8,128)(2,1)S(1)}, bf16[128,4096]{1,0:T(8,128)(2,1)S(1)}, u32[]{:S(2)}, u32[]{:S(2)}) collective-permute-start(bf16[128,4096]{1,0:T(8,128)(2,1)S(1)} %pad_maximum_fusion.2), channel_id=1, source_target_pairs={{0,4},{4,0},{1,5},{5,1},{2,6},{6,2},{3,7},{7,3},{8,12},{12,8},{9,1... | collective-permute-start | bytes 3145736 | tf_op jit(solution)/shard_map/ppermute | solution.py:22
  135.8 0.5 fusion.7
  136.3 45.5 %collective-permute-done.3 = bf16[128,4096]{1,0:T(8,128)(2,1)S(1)} collective-permute-done((bf16[128,4096]{1,0:T(8,128)(2,1)S(1)}, bf16[128,4096]{1,0:T(8,128)(2,1)S(1)}, u32[]{:S(2)}, u32[]{:S(2)}) %collective-permute-start.3) | collective-permute-done | bytes 1048608 | tf_op jit(solution)/shard_map/ppermute | solution.py:22
  181.8 0.5 convolution_add_fusion
  182.5 0.4 copy-done.1
  183.0 0.3 convolution_convert_fusion
  183.5 7.2 %collective-permute-start.4 = (bf16[2,8,4096]{2,0,1:T(2,128)(2,1)S(1)}, bf16[2,8,4096]{2,0,1:T(2,128)(2,1)S(1)}, u32[]{:S(2)}, u32[]{:S(2)}) collective-permute-start(bf16[2,8,4096]{2,0,1:T(2,128)(2,1)S(1)} %copy.9), channel_id=1, source_target_pairs={{0,16},{16,32},{32,48},{48,64},{64,80},{80,96},{96,112},{112,128},... | collective-permute-start | bytes 393224 | tf_op jit(solution)/shard_map/ppermute | solution.py:30
  190.8 1.9 collective-permute-start.5
  193.0 9.7 %collective-permute-done.5 = bf16[2,8,4096]{2,0,1:T(2,128)(2,1)S(1)} collective-permute-done((bf16[2,8,4096]{2,0,1:T(2,128)(2,1)S(1)}, bf16[2,8,4096]{2,0,1:T(2,128)(2,1)S(1)}, u32[]{:S(2)}, u32[]{:S(2)}) %collective-permute-start.5) | collective-permute-done | bytes 131104 | tf_op jit(solution)/shard_map/ppermute | solution.py:33
  203.0 7.7 %collective-permute-start.6 = (bf16[12,2,4096]{2,0,1:T(8,128)(2,1)S(1)}, bf16[12,2,4096]{2,0,1:T(8,128)(2,1)S(1)}, u32[]{:S(2)}, u32[]{:S(2)}) collective-permute-start(bf16[12,2,4096]{2,0,1:T(8,128)(2,1)S(1)} %get-tuple-element.31), channel_id=1, source_target_pairs={{0,1},{1,2},{2,3},{3,4},{4,5},{5,6},{6,7},{7,8},{8,9},{9,10},{10,1... | collective-permute-start | bytes 589832 | tf_op jit(solution)/shard_map/ppermute | solution.py:30
  210.7 1.9 collective-permute-start.7
  213.3 0.7 collective-permute-done.6
  214.0 5.0 %collective-permute-done.7 = bf16[12,2,4096]{2,0,1:T(8,128)(2,1)S(1)} collective-permute-done((bf16[12,2,4096]{2,0,1:T(8,128)(2,1)S(1)}, bf16[12,2,4096]{2,0,1:T(8,128)(2,1)S(1)}, u32[]{:S(2)}, u32[]{:S(2)}) %collective-permute-start.7) | collective-permute-done | bytes 196640 | tf_op jit(solution)/shard_map/ppermute | solution.py:33
  219.0 0.5 maximum_convert_fusion
  219.6 0.6 slice_add_fusion
  220.2 0.3 fusion.2
  220.5 1.1 copy.12
  (19 shorter events, 2.5 us)
Async XLA Ops:
  0.0 55.1 %collective-permute-start = (bf16[128,4096]{1,0:T(8,128)(2,1)}, bf16[128,4096]{1,0:T(8,128)(2,1)S(1)}, u32[]{:S(2)}, u32[]{:S(2)}) collective-permute-start(bf16[128,4096]{1,0:T(8,128)(2,1)} %bitcast.58), channel_id=1, source_target_pairs={{0,256},{256,0},{16,272},{272,16},{32,288},{288,32},{48,304},{304,... | collective-permute-start | bytes 3145736 | tf_op jit(solution)/shard_map/ppermute | solution.py:22
  56.0 26.0 %collective-permute-start.1 = (bf16[128,4096]{1,0:T(8,128)(2,1)S(1)}, bf16[128,4096]{1,0:T(8,128)(2,1)S(1)}, u32[]{:S(2)}, u32[]{:S(2)}) collective-permute-start(bf16[128,4096]{1,0:T(8,128)(2,1)S(1)} %pad_maximum_fusion), channel_id=1, source_target_pairs={{0,8},{8,0},{1,9},{9,1},{2,10},{10,2},{3,11},{11,3},{4,12},{12,4},... | collective-permute-start | bytes 3145736 | tf_op jit(solution)/shard_map/ppermute | solution.py:22
  82.9 47.3 %collective-permute-start.2 = (bf16[128,4096]{1,0:T(8,128)(2,1)S(1)}, bf16[128,4096]{1,0:T(8,128)(2,1)S(1)}, u32[]{:S(2)}, u32[]{:S(2)}) collective-permute-start(bf16[128,4096]{1,0:T(8,128)(2,1)S(1)} %pad_maximum_fusion.1), channel_id=1, source_target_pairs={{0,128},{128,0},{16,144},{144,16},{32,160},{160,32},{48,176},{176,... | collective-permute-start | bytes 3145736 | tf_op jit(solution)/shard_map/ppermute | solution.py:22
  130.6 5.2 %copy-start = (bf16[64,64]{1,0:T(8,128)(2,1)S(1)}, bf16[64,64]{1,0:T(8,128)(2,1)}, u32[]{:S(2)}) copy-start(bf16[64,64]{1,0:T(8,128)(2,1)} %param.14) | copy-start | bytes 24580
  131.0 50.8 %collective-permute-start.3 = (bf16[128,4096]{1,0:T(8,128)(2,1)S(1)}, bf16[128,4096]{1,0:T(8,128)(2,1)S(1)}, u32[]{:S(2)}, u32[]{:S(2)}) collective-permute-start(bf16[128,4096]{1,0:T(8,128)(2,1)S(1)} %pad_maximum_fusion.2), channel_id=1, source_target_pairs={{0,4},{4,0},{1,5},{5,1},{2,6},{6,2},{3,7},{7,3},{8,12},{12,8},{9,1... | collective-permute-start | bytes 3145736 | tf_op jit(solution)/shard_map/ppermute | solution.py:22
  182.2 0.7 copy-start.1
  183.5 9.6 %collective-permute-start.4 = (bf16[2,8,4096]{2,0,1:T(2,128)(2,1)S(1)}, bf16[2,8,4096]{2,0,1:T(2,128)(2,1)S(1)}, u32[]{:S(2)}, u32[]{:S(2)}) collective-permute-start(bf16[2,8,4096]{2,0,1:T(2,128)(2,1)S(1)} %copy.9), channel_id=1, source_target_pairs={{0,16},{16,32},{32,48},{48,64},{64,80},{80,96},{96,112},{112,128},... | collective-permute-start | bytes 393224 | tf_op jit(solution)/shard_map/ppermute | solution.py:30
  190.8 11.9 %collective-permute-start.5 = (bf16[2,8,4096]{2,0,1:T(2,128)(2,1)S(1)}, bf16[2,8,4096]{2,0,1:T(2,128)(2,1)S(1)}, u32[]{:S(2)}, u32[]{:S(2)}) collective-permute-start(bf16[2,8,4096]{2,0,1:T(2,128)(2,1)S(1)} %copy.10), channel_id=1, source_target_pairs={{16,0},{32,16},{48,32},{64,48},{80,64},{96,80},{112,96},{128,112},... | collective-permute-start | bytes 393224 | tf_op jit(solution)/shard_map/ppermute | solution.py:33
  203.0 11.0 %collective-permute-start.6 = (bf16[12,2,4096]{2,0,1:T(8,128)(2,1)S(1)}, bf16[12,2,4096]{2,0,1:T(8,128)(2,1)S(1)}, u32[]{:S(2)}, u32[]{:S(2)}) collective-permute-start(bf16[12,2,4096]{2,0,1:T(8,128)(2,1)S(1)} %get-tuple-element.31), channel_id=1, source_target_pairs={{0,1},{1,2},{2,3},{3,4},{4,5},{5,6},{6,7},{7,8},{8,9},{9,10},{10,1... | collective-permute-start | bytes 589832 | tf_op jit(solution)/shard_map/ppermute | solution.py:30
  210.7 8.3 %collective-permute-start.7 = (bf16[12,2,4096]{2,0,1:T(8,128)(2,1)S(1)}, bf16[12,2,4096]{2,0,1:T(8,128)(2,1)S(1)}, u32[]{:S(2)}, u32[]{:S(2)}) collective-permute-start(bf16[12,2,4096]{2,0,1:T(8,128)(2,1)S(1)} %get-tuple-element.32), channel_id=1, source_target_pairs={{1,0},{2,1},{3,2},{4,3},{5,4},{6,5},{7,6},{8,7},{9,8},{10,9},{11,1... | collective-permute-start | bytes 589832 | tf_op jit(solution)/shard_map/ppermute | solution.py:33
where the time goes:
time: 222 us
  waiting for transfers between devices  171 us (77%)
  starting transfers between devices  36.2 us (16%)
  matrix products  5.39 us (2%)
  other arithmetic  4.94 us (2%)
  local copies, waits for them, and re-layouts  2.99 us (1%)
    ppermute x4, waiting for transfers between devices, swapped(): return lax.ppermute(block, axis, route)  156 us
    ppermute x4, starting transfers between devices, swapped(): return lax.ppermute(block, axis, route)  17.4 us
    ppermute x2, starting transfers between devices, with_halo(): lax.ppermute(lax.slice_in_dim(block, block.shape[dim] - width, None, axis...  14.9 us
    ppermute x2, waiting for transfers between devices, with_halo(): lax.ppermute(lax.slice_in_dim(block, 0, width, axis=dim), axis, backward)  14.7 us
  transfers between devices with their start and end apart: 8, of which 7 were waited for; matrix products, arithmetic and copies ran while one was open for 3% of the time, Pallas kernels for 0%

commit v1 on v0

v1 whole, which is shorter than its diff:
```python
import functools
import math

import jax
import jax.numpy as jnp
import numpy as np
from jax import lax
from jax.experimental import pallas as pl
from jax.experimental.pallas import tpu as pltpu
from jax.sharding import Mesh
from jax.sharding import PartitionSpec as P

LEVELS = 4
VGRID = 4096
K = 64
TILE = 8
COLS = 4096
BOXES = 64
ZBOX = 8
YBOX = 8
HALF = 64
LANES = 128
WIDE = YBOX * HALF
ROWS = K + 8
TWO_PI = 2.0 * math.pi
GROUP = ("zh", "zl", "y")


def turn(x):
    return jnp.concatenate([x[..., HALF:], x[..., :HALF]], axis=-1)


def lane_low(shape):
    return lax.broadcasted_iota(jnp.int32, shape, len(shape) - 1) % LANES < HALF


def pack_kernel(info_ref, window_ref, frame_ref, velocity_ref, source_ref, out_ref):
    step = pl.program_id(0)
    low = lane_low((K, LANES))
    small_low = lane_low((8, LANES))
    own_row = lax.broadcasted_iota(jnp.int32, (8, LANES), 0) == info_ref[0]
    width = window_ref[0].astype(jnp.float32)
    tiles = source_ref.shape[-1] // LANES
    for tile in range(tiles):
        lanes = pl.ds(tile * LANES, LANES)
        real = source_ref[0, :, lanes].astype(jnp.float32)
        imag = source_ref[1, :, lanes].astype(jnp.float32)
        out_ref[2 * tile, :K, :] = jnp.where(low, real, turn(imag)).astype(jnp.bfloat16)
        out_ref[2 * tile + 1, :K, :] = jnp.where(low, turn(real), imag).astype(jnp.bfloat16)
        frame = frame_ref[step * (tiles // 2) + tile // 2]
        velocity = velocity_ref[:, pl.ds((tile % 2) * LANES, LANES)]
        product = jnp.broadcast_to((frame * velocity) & (VGRID - 1), (8, LANES))
        high_part = (product >> 6).astype(jnp.float32)
        low_part = (product & 63).astype(jnp.float32)
        even = jnp.where(small_low, high_part, turn(low_part))
        odd = jnp.where(small_low, turn(high_part), low_part)
        out_ref[2 * tile, K:, :] = jnp.where(own_row, even, width).astype(jnp.bfloat16)
        out_ref[2 * tile + 1, K:, :] = jnp.where(own_row, odd, width).astype(jnp.bfloat16)


def pack(info, window, frame_index, velocity_index, sources):
    steps = 4
    width = COLS // steps
    return pl.pallas_call(
        pack_kernel,
        grid=(steps,),
        out_shape=jax.ShapeDtypeStruct((BOXES, ROWS, LANES), jnp.bfloat16),
        in_specs=[
            pl.BlockSpec(memory_space=pltpu.SMEM),
            pl.BlockSpec(memory_space=pltpu.SMEM),
            pl.BlockSpec(memory_space=pltpu.SMEM),
            pl.BlockSpec((1, 2 * LANES), lambda s: (0, 0)),
            pl.BlockSpec((2, K, width), lambda s: (0, 0, s)),
        ],
        out_specs=pl.BlockSpec((BOXES // steps, ROWS, LANES), lambda s: (s, 0, 0)),
        cost_estimate=pl.CostEstimate(flops=4 << 20, bytes_accessed=2 << 20, transcendentals=0),
        name="pack",
    )(info, window, frame_index, velocity_index, sources)


def butterfly_kernel(
    info_ref,
    got_ref,
    mats_ref,
    eval_ref,
    picture_ref,
    below_ref,
    above_ref,
    width_ref,
    state_ref,
    cos_ref,
    sin_ref,
):
    low = lane_low((K, LANES))
    small_low = lane_low((8, LANES))
    row = lax.broadcasted_iota(jnp.int32, (8, LANES), 0)
    for pair in range(YBOX // 2):
        lanes = pl.ds(pair * LANES, LANES)
        indices = []
        widths = []
        for y in (2 * pair, 2 * pair + 1):
            index = jnp.zeros((8, LANES), jnp.float32)
            width = jnp.zeros((8, LANES), jnp.float32)
            for z in range(ZBOX):
                extra = got_ref[z * YBOX + y, K:, :].astype(jnp.float32)
                index = jnp.where(row == z, extra, index)
                width = jnp.where(row == (z + 1) % ZBOX, extra, width)
            indices.append(index)
            widths.append(width)
        high_part = jnp.where(small_low, indices[0], turn(indices[1]))
        low_part = jnp.where(small_low, turn(indices[0]), indices[1])
        width_ref[:, lanes] = jnp.where(small_low, widths[0], widths[1])
        angle = (TWO_PI / VGRID) * (64.0 * high_part + low_part)
        cosine = jnp.cos(angle)
        sine = jnp.sin(angle)
        cos_now, sin_now = cosine, sine
        for level in range(LEVELS):
            cos_ref[level, :, lanes] = cos_now
            sin_ref[level, :, lanes] = sin_now
            if level + 1 < LEVELS:
                cos_now, sin_now = (
                    cos_now * cosine - sin_now * sine,
                    sin_now * cosine + cos_now * sine,
                )
    for z in range(ZBOX):
        for pair in range(YBOX // 2):
            lanes = pl.ds(pair * LANES, LANES)
            even = got_ref[z * YBOX + 2 * pair, :K, :].astype(jnp.float32)
            odd = got_ref[z * YBOX + 2 * pair + 1, :K, :].astype(jnp.float32)
            state_ref[z, :K, lanes] = jnp.where(low, even, turn(odd)).astype(jnp.bfloat16)
            state_ref[z, K:, lanes] = jnp.where(low, turn(even), odd).astype(jnp.bfloat16)

    def rotated(level, z, lanes, total):
        cosine = cos_ref[level, pl.ds(z, 1), lanes]
        sine = sin_ref[level, pl.ds(z, 1), lanes]
        real, imag = total[:K], total[K:]
        state_ref[z, :K, lanes] = (cosine * real - sine * imag).astype(jnp.bfloat16)
        state_ref[z, K:, lanes] = (sine * real + cosine * imag).astype(jnp.bfloat16)

    for level, bit in ((0, 4), (1, 1), (2, 2)):
        for z in range(ZBOX):
            if z & bit:
                continue
            for part in range(2):
                lanes = pl.ds(part * 256, 256)
                both = jnp.concatenate([state_ref[z, :, lanes], state_ref[z | bit, :, lanes]], 0)
                total = jnp.dot(mats_ref[level], both, preferred_element_type=jnp.float32)
                rotated(level, z, lanes, total[: 2 * K])
                rotated(level, z | bit, lanes, total[2 * K :])
    for z in range(ZBOX):
        first, second = pl.ds(0, 256), pl.ds(256, 256)
        both = jnp.concatenate([state_ref[z, :, first], state_ref[z, :, second]], 0)
        total = jnp.dot(mats_ref[3], both, preferred_element_type=jnp.float32)
        rotated(3, z, first, total[: 2 * K])
        rotated(3, z, second, total[2 * K :])
    for z in range(ZBOX):
        picture_ref[z] = jnp.dot(
            eval_ref[...], state_ref[z], preferred_element_type=jnp.float32
        ).astype(jnp.bfloat16)
    last = info_ref[1] == 7
    first = info_ref[1] == 0
    nothing = jnp.zeros((16, WIDE), jnp.bfloat16)
    for z in range(ZBOX):

        @pl.when(last)
        def _():
            below_ref[z] = picture_ref[z - 2, 48:, :] if z >= 2 else nothing

        @pl.when(jnp.logical_not(last))
        def _():
            below_ref[z] = picture_ref[z, 48:, :]

        @pl.when(first)
        def _():
            above_ref[z] = picture_ref[z + 2, :16, :] if z + 2 < ZBOX else nothing

        @pl.when(jnp.logical_not(first))
        def _():
            above_ref[z] = picture_ref[z, :16, :]


def butterfly(info, got, mats, evaluate):
    whole = pl.BlockSpec(memory_space=pltpu.VMEM)
    return pl.pallas_call(
        butterfly_kernel,
        out_shape=(
            jax.ShapeDtypeStruct((ZBOX, K, WIDE), jnp.bfloat16),
            jax.ShapeDtypeStruct((ZBOX, 16, WIDE), jnp.bfloat16),
            jax.ShapeDtypeStruct((ZBOX, 16, WIDE), jnp.bfloat16),
            jax.ShapeDtypeStruct((ZBOX, WIDE), jnp.float32),
        ),
        in_specs=[pl.BlockSpec(memory_space=pltpu.SMEM), whole, whole, whole],
        out_specs=(whole, whole, whole, whole),
        scratch_shapes=[
            pltpu.VMEM((ZBOX, 2 * K, WIDE), jnp.bfloat16),
            pltpu.VMEM((LEVELS, ZBOX, WIDE), jnp.float32),
            pltpu.VMEM((LEVELS, ZBOX, WIDE), jnp.float32),
        ],
        cost_estimate=pl.CostEstimate(flops=2 << 30, bytes_accessed=3 << 20, transcendentals=8192),
        name="butterfly",
    )(info, got, mats, evaluate)


def smooth_kernel(picture_ref, below_ref, above_ref, width_ref, sums_ref, out_ref):
    rows = K + 32
    low = lane_low((rows, LANES))
    half_low = lane_low((32, LANES))
    upper = lax.broadcasted_iota(jnp.int32, (rows, LANES), 0) % 8 >= 4
    nothing = jnp.zeros((rows, LANES), jnp.float32)

    def tile(z, pair):
        lanes = pl.ds(pair * LANES, LANES)
        parts = [below_ref[z, :, lanes], picture_ref[z, :, lanes], above_ref[z, :, lanes]]
        return jnp.concatenate(parts, axis=0).astype(jnp.float32)

    for zh in range(ZBOX // 2):
        line = [(2 * zh + i // 4, i % 4) for i in range(8)]
        before, here = nothing, tile(*line[0])
        for i, (z, pair) in enumerate(line):
            after = tile(*line[i + 1]) if i + 1 < len(line) else nothing
            left = jnp.where(low, here, before)
            right = jnp.where(low, after, here)
            beside = turn(jnp.where(upper, left, right))
            field = jnp.concatenate([here, beside], axis=0).astype(jnp.bfloat16)
            sums = jnp.dot(sums_ref[...], field, preferred_element_type=jnp.float32)
            wide = width_ref[pl.ds((z + 1) % ZBOX, 1), pl.ds(pair * LANES, LANES)] > 1.5
            chosen = jnp.where(wide, sums[K:] / 25.0, sums[:K] / 9.0)
            top, bottom = chosen[:32], chosen[32:]
            box = z * YBOX + 2 * pair
            out_ref[box] = jnp.where(half_low, top, turn(bottom)).astype(jnp.bfloat16)
            out_ref[box + 1] = jnp.where(half_low, turn(top), bottom).astype(jnp.bfloat16)
            before, here = here, after


def smooth(picture, below, above, widths, sums):
    whole = pl.BlockSpec(memory_space=pltpu.VMEM)
    return pl.pallas_call(
        smooth_kernel,
        out_shape=jax.ShapeDtypeStruct((BOXES, 32, LANES), jnp.bfloat16),
        in_specs=[whole] * 5,
        out_specs=whole,
        cost_estimate=pl.CostEstimate(flops=1 << 28, bytes_accessed=2 << 20, transcendentals=0),
        name="smooth",
    )(picture, below, above, widths, sums)


def unpack_kernel(got_ref, out_ref):
    low = lane_low((32, LANES))
    for tile in range(out_ref.shape[-1] // LANES):
        lanes = pl.ds(tile * LANES, LANES)
        even = got_ref[2 * tile].astype(jnp.float32)
        odd = got_ref[2 * tile + 1].astype(jnp.float32)
        out_ref[:32, lanes] = jnp.where(low, even, turn(odd)).astype(jnp.bfloat16)
        out_ref[32:, lanes] = jnp.where(low, turn(even), odd).astype(jnp.bfloat16)


def unpack(got):
    steps = 2
    return pl.pallas_call(
        unpack_kernel,
        grid=(steps,),
        out_shape=jax.ShapeDtypeStruct((K, COLS), jnp.bfloat16),
        in_specs=[pl.BlockSpec((BOXES // steps, 32, LANES), lambda s: (s, 0, 0))],
        out_specs=pl.BlockSpec((K, COLS // steps), lambda s: (0, s)),
        cost_estimate=pl.CostEstimate(flops=1 << 20, bytes_accessed=1 << 20, transcendentals=0),
        name="unpack",
    )(got)


def box_sums():
    sums = np.zeros((2, TILE, TILE, 2, TILE + 4, TILE), np.float32)
    for reach in (1, 2):
        for a in range(TILE):
            for b in range(TILE):
                for x in range(TILE + 4):
                    for y in range(TILE):
                        if abs(x - 2 - a) > reach:
                            continue
                        other = y - TILE if y >= 4 else y + TILE
                        sums[reach - 1, a, b, 0, x, y] = abs(y - b) <= reach
                        sums[reach - 1, a, b, 1, x, y] = abs(other - b) <= reach
    return sums.reshape(2 * K, 2 * (K + 32))


def blocks(real_part, imag_part):
    upper = jnp.concatenate([real_part, -imag_part], axis=-1)
    lower = jnp.concatenate([imag_part, real_part], axis=-1)
    return jnp.concatenate([upper, lower], axis=-2)


def on_device(
    sources, translate_re, translate_im, frame_index, velocity_index, eval_re, eval_im, window
):
    z = lax.axis_index("zh") * 2 + lax.axis_index("zl")
    place = lax.broadcasted_iota(jnp.int32, (2,), 0)
    info = jnp.where(place == 0, z, lax.axis_index("xc"))
    message = pack(
        info, window.reshape(1), frame_index.reshape(16), velocity_index.reshape(1, 256), sources[0, 0]
    )
    got = lax.all_to_all(message, GROUP, 0, 0, tiled=True)
    own = blocks(translate_re[:, :, 0], translate_im[:, :, 0])
    other = blocks(translate_re[:, :, 1], translate_im[:, :, 1])
    mats = jnp.concatenate(
        [
            jnp.concatenate([own[:, 0], other[:, 0]], axis=-1),
            jnp.concatenate([other[:, 1], own[:, 1]], axis=-1),
        ],
        axis=-2,
    )
    evaluate = jnp.concatenate([eval_re, -eval_im], axis=1)
    picture, last_rows, first_rows, widths = butterfly(info, got, mats, evaluate)
    below = lax.ppermute(last_rows, "xc", [(i, (i + 1) % 8) for i in range(8)])
    above = lax.ppermute(first_rows, "xc", [(i, (i + 7) % 8) for i in range(8)])
    smoothed = smooth(picture, below, above, widths, jnp.asarray(box_sums(), jnp.bfloat16))
    back = lax.all_to_all(smoothed, GROUP, 0, 0, tiled=True)
    return unpack(back).reshape(TILE, TILE, COLS)


def solution(mesh):
    fine = Mesh(mesh.devices.reshape(4, 8, 2, 8), ("zh", "xc", "zl", "y"))
    box = (("zh", "xc"), ("zl", "y"))
    return jax.shard_map(
        on_device,
        mesh=fine,
        in_specs=(
            P(*box, None, None, None),
            P(),
            P(),
            P(*box, None),
            P(*box, None),
            P(),
            P(),
            P(*box),
        ),
        out_specs=P(*box, None),
        check_vma=False,
    )
```

time: 222 us -> 97.7 us (0.44)
  the two profiles are of different devices: /device:TPU:159 before, /device:TPU:8 now
where the time goes in v1:
time: 97.7 us; the launch traced here: 97.3 us
  waiting for transfers between devices  32.8 us (34%)
  blocking collectives  26.8 us (27%)
  starting transfers between devices  19.7 us (20%)
  Pallas kernels  12.9 us (13%)
  other arithmetic  2.37 us (2%)
  local copies, waits for them, and re-layouts  1.89 us (2%)
    all_to_all x1, waiting for transfers between devices, on_device(): got = lax.all_to_all(message, GROUP, 0, 0, tiled=True)  29.9 us
    all_to_all x1, blocking collectives, on_device(): back = lax.all_to_all(smoothed, GROUP, 0, 0, tiled=True)  26.8 us
    all_to_all x1, starting transfers between devices, on_device(): got = lax.all_to_all(message, GROUP, 0, 0, tiled=True)  16.7 us
    pallas_call x1, Pallas kernels, butterfly(): pl.pallas_call(butterfly_kernel, out_shape=(jax.ShapeDtypeStruct((ZBOX, K...  4.49 us
    pallas_call x1, Pallas kernels, pack(): pl.pallas_call(pack_kernel, grid=(steps,), out_shape=jax.ShapeDtypeStruct...  3.66 us
    ppermute x1, starting transfers between devices, on_device(): above = lax.ppermute(first_rows, 'xc', [(i, (i + 7) % 8) for i in range(8)])  2.95 us
    ppermute x1, waiting for transfers between devices, on_device(): below = lax.ppermute(last_rows, 'xc', [(i, (i + 1) % 8) for i in range(8)])  2.86 us
    pallas_call x1, Pallas kernels, smooth(): pl.pallas_call(smooth_kernel, out_shape=jax.ShapeDtypeStruct((BOXES, 32,...  2.82 us
  transfers between devices with their start and end apart: 3, of which 2 were waited for; matrix products, arithmetic and copies ran while one was open for 2% of the time, Pallas kernels for 0%

profile of v1, /device:TPU:8, one launch (start us, length us, event | category | flops | bytes accessed | tf_op | source)
XLA Modules:
  0.0 97.3 jit_solution(12493812490296507520)
XLA Ops:
  0.7 0.5 compare_select_fusion.info_ref
  1.1 3.7 %pack.1 = bf16[64,72,128]{2,1,0:T(8,128)(2,1)} custom-call(s32[2]{0:T(128)} %compare_select_fusion.info_ref, s32[1]{0:T(128)} %bitcast.25.window_ref, s32[16]{0:T(128)} %bitcast.28, s32[1,256]{1,0:T(1,128)} %bitcast.27, bf16[2,64,4096]{2,1,0:T(8,128)(2,1)} %bitcast.26), custom_call_target="tpu_custom_call" | custom-call | flops 4194304 | bytes 2097152 | tf_op jit(solution)/shard_map/pack/pallas_call | solution.py:64
  4.8 0.0 copy-start.6
  4.8 0.0 copy-start.5
  4.8 0.0 copy-start.1
  4.8 0.0 copy-start.2
  4.8 16.7 %all-to-all-start = ((bf16[64,72,128]{2,1,0:T(8,128)(2,1)}), bf16[64,72,128]{2,1,0:T(8,128)(2,1)S(1)}, u32[]{:S(2)}, u32[]{:S(2)}) async-start(bf16[64,72,128]{2,1,0:T(8,128)(2,1)} %pack.1), calls=%async_computation | async-start | bytes 2359296 | tf_op jit(solution)/shard_map/all_to_all | solution.py:300
  21.6 0.0 copy-done.6
  21.6 0.0 copy-done.5
  21.6 0.7 pad_maximum_fusion.eval_ref
  22.3 0.0 copy-done.1
  22.3 0.0 copy-done.2
  22.4 0.2 maximum_maximum_fusion.1
  22.6 0.2 maximum_maximum_fusion.2
  22.8 0.9 maximum_maximum_fusion.mats_ref
  23.7 29.9 %all-to-all-done.got_ref = bf16[64,72,128]{2,1,0:T(8,128)(2,1)S(1)} async-done(((bf16[64,72,128]{2,1,0:T(8,128)(2,1)}), bf16[64,72,128]{2,1,0:T(8,128)(2,1)S(1)}, u32[]{:S(2)}, u32[]{:S(2)}) %all-to-all-start) | async-done | bytes 1179680 | tf_op jit(solution)/shard_map/all_to_all | solution.py:300
  53.6 0.0 copy-start
  53.6 1.1 %copy-done = bf16[64,72,128]{2,1,0:T(8,128)(2,1)} copy-done((bf16[64,72,128]{2,1,0:T(8,128)(2,1)}, bf16[64,72,128]{2,1,0:T(8,128)(2,1)S(1)}, u32[]{:S(2)}) %copy-start) | copy-done | bytes 1179672
  54.6 4.5 %butterfly.1 = (bf16[8,64,512]{2,1,0:T(8,128)(2,1)}, bf16[8,16,512]{2,1,0:T(8,128)(2,1)}, bf16[8,16,512]{2,1,0:T(8,128)(2,1)}, f32[8,512]{1,0:T(8,128)}) custom-call(s32[2]{0:T(128)} %compare_select_fusion.info_ref, bf16[64,72,128]{2,1,0:T(8,128)(2,1)} %copy-done, bf16[4,256,256]{2,1,0:T(8,128)(2,1)} %maximum_maximum_fusion.mats_ref, ...), custom_call_target="tpu_custom_call" | custom-call | flops 2147483648 | bytes 3145728 | tf_op jit(solution)/shard_map/butterfly/pallas_call | solution.py:184
  59.1 0.0 collective-permute-start
  59.1 3.0 %collective-permute-start.1 = (bf16[8,16,512]{2,1,0:T(8,128)(2,1)}, bf16[8,16,512]{2,1,0:T(8,128)(2,1)S(1)}, u32[]{:S(2)}, u32[]{:S(2)}) collective-permute-start(bf16[8,16,512]{2,1,0:T(8,128)(2,1)} %get-tuple-element.11), channel_id=1, source_target_pairs={{0,112},{16,0},{32,16},{48,32},{64,48},{80,64},{96,80},{112,96},{1... | collective-permute-start | bytes 393224 | tf_op jit(solution)/shard_map/ppermute | solution.py:313
  62.1 2.9 %collective-permute-done.below_ref = bf16[8,16,512]{2,1,0:T(8,128)(2,1)S(1)} collective-permute-done((bf16[8,16,512]{2,1,0:T(8,128)(2,1)}, bf16[8,16,512]{2,1,0:T(8,128)(2,1)S(1)}, u32[]{:S(2)}, u32[]{:S(2)}) %collective-permute-start) | collective-permute-done | bytes 131104 | tf_op jit(solution)/shard_map/ppermute | solution.py:312
  65.0 0.0 copy-start.3
  65.0 0.0 collective-permute-done.1.above_ref
  65.0 0.0 copy-start.4
  65.0 0.7 copy-done.3
  65.6 0.0 copy-done.4
  65.7 2.8 %smooth.1 = bf16[64,32,128]{2,1,0:T(8,128)(2,1)} custom-call(bf16[8,64,512]{2,1,0:T(8,128)(2,1)} %get-tuple-element.9.picture_ref, bf16[8,16,512]{2,1,0:T(8,128)(2,1)} %copy-done.3, bf16[8,16,512]{2,1,0:T(8,128)(2,1)} %copy-done.4, f32[8,512]{1,0:T(8,128)} %get-tuple-element.12.width_ref, bf16[128,192]{1,0:T(8,128)(2,1)} %constant.21.clone.sums_ref), custom_call_target="tpu_custom_call" | custom-call | flops 268435456 | bytes 2097152 | tf_op jit(solution)/shard_map/smooth/pallas_call | solution.py:237
  68.5 26.8 %all_to_all.10.got_ref = bf16[64,32,128]{2,1,0:T(8,128)(2,1)} all-to-all(bf16[64,32,128]{2,1,0:T(8,128)(2,1)} %smooth.1), channel_id=1, replica_groups=mesh['zh'=4,'xc'=8,'zl'=2,'y'=8] {'zh','zl','y'}, dimensions={0} | all-to-all | bytes 1048576 | tf_op jit(solution)/shard_map/all_to_all | solution.py:315
  95.3 1.9 %unpack.1 = bf16[64,4096]{1,0:T(8,128)(2,1)} custom-call(bf16[64,32,128]{2,1,0:T(8,128)(2,1)} %all_to_all.10.got_ref), custom_call_target="tpu_custom_call" | custom-call | flops 1048576 | bytes 1048576 | tf_op jit(solution)/shard_map/unpack/pallas_call | solution.py:259
  (8 shorter events, 0.2 us)
Async XLA Ops:
  4.8 16.8 %copy-start.6 = (bf16[64,64]{1,0:T(8,128)(2,1)S(1)}, bf16[64,64]{1,0:T(8,128)(2,1)}, u32[]{:S(2)}) copy-start(bf16[64,64]{1,0:T(8,128)(2,1)} %param.15) | copy-start | bytes 24580
  4.8 16.8 %copy-start.5 = (bf16[64,64]{1,0:T(8,128)(2,1)S(1)}, bf16[64,64]{1,0:T(8,128)(2,1)}, u32[]{:S(2)}) copy-start(bf16[64,64]{1,0:T(8,128)(2,1)} %param.14) | copy-start | bytes 24580
  4.8 17.5 %copy-start.1 = (bf16[4,2,2,64,64]{4,3,2,1,0:T(8,128)(2,1)S(1)}, bf16[4,2,2,64,64]{4,3,2,1,0:T(8,128)(2,1)}, u32[]{:S(2)}) copy-start(bf16[4,2,2,64,64]{4,3,2,1,0:T(8,128)(2,1)} %param.10) | copy-start | bytes 393220
  4.8 17.5 %copy-start.2 = (bf16[4,2,2,64,64]{4,3,2,1,0:T(8,128)(2,1)S(1)}, bf16[4,2,2,64,64]{4,3,2,1,0:T(8,128)(2,1)}, u32[]{:S(2)}) copy-start(bf16[4,2,2,64,64]{4,3,2,1,0:T(8,128)(2,1)} %param.11) | copy-start | bytes 393220
  4.8 48.8 %all-to-all-start = ((bf16[64,72,128]{2,1,0:T(8,128)(2,1)}), bf16[64,72,128]{2,1,0:T(8,128)(2,1)S(1)}, u32[]{:S(2)}, u32[]{:S(2)}) async-start(bf16[64,72,128]{2,1,0:T(8,128)(2,1)} %pack.1), calls=%async_computation | async-start | bytes 2359296 | tf_op jit(solution)/shard_map/all_to_all | solution.py:300
  53.6 1.1 %copy-start = (bf16[64,72,128]{2,1,0:T(8,128)(2,1)}, bf16[64,72,128]{2,1,0:T(8,128)(2,1)S(1)}, u32[]{:S(2)}) copy-start(bf16[64,72,128]{2,1,0:T(8,128)(2,1)S(1)} %all-to-all-done.got_ref) | copy-start | bytes 3538948
  59.1 5.8 %collective-permute-start = (bf16[8,16,512]{2,1,0:T(8,128)(2,1)}, bf16[8,16,512]{2,1,0:T(8,128)(2,1)S(1)}, u32[]{:S(2)}, u32[]{:S(2)}) collective-permute-start(bf16[8,16,512]{2,1,0:T(8,128)(2,1)} %get-tuple-element.10), channel_id=1, source_target_pairs={{0,16},{16,32},{32,48},{48,64},{64,80},{80,96},{96,112},{112,0},{1... | collective-permute-start | bytes 393224 | tf_op jit(solution)/shard_map/ppermute | solution.py:312
  59.1 5.8 %collective-permute-start.1 = (bf16[8,16,512]{2,1,0:T(8,128)(2,1)}, bf16[8,16,512]{2,1,0:T(8,128)(2,1)S(1)}, u32[]{:S(2)}, u32[]{:S(2)}) collective-permute-start(bf16[8,16,512]{2,1,0:T(8,128)(2,1)} %get-tuple-element.11), channel_id=1, source_target_pairs={{0,112},{16,0},{32,16},{48,32},{64,48},{80,64},{96,80},{112,96},{1... | collective-permute-start | bytes 393224 | tf_op jit(solution)/shard_map/ppermute | solution.py:313
  65.0 0.7 copy-start.3
  65.0 0.7 copy-start.4

commit v2 on v1

--- a/solution.py
+++ b/solution.py
@@ -21,7 +21,7 @@
 HALF = 64
 LANES = 128
 WIDE = YBOX * HALF
-ROWS = K + 8
+ROWS = K + 2
 TWO_PI = 2.0 * math.pi
 GROUP = ("zh", "zl", "y")
 
@@ -34,53 +34,51 @@
     return lax.broadcasted_iota(jnp.int32, shape, len(shape) - 1) % LANES < HALF
 
 
-def pack_kernel(info_ref, window_ref, frame_ref, velocity_ref, source_ref, out_ref):
+def pack_kernel(window_ref, frame_ref, velocity_ref, source_ref, out_ref):
     step = pl.program_id(0)
-    low = lane_low((K, LANES))
-    small_low = lane_low((8, LANES))
-    own_row = lax.broadcasted_iota(jnp.int32, (8, LANES), 0) == info_ref[0]
-    width = window_ref[0].astype(jnp.float32)
+    low = lane_low((1, LANES))
     tiles = source_ref.shape[-1] // LANES
+    out = out_ref.reshape(2 * tiles, ROWS, LANES)
+    width = jnp.full((1, LANES), window_ref[0].astype(jnp.float32))
     for tile in range(tiles):
         lanes = pl.ds(tile * LANES, LANES)
-        real = source_ref[0, :, lanes].astype(jnp.float32)
-        imag = source_ref[1, :, lanes].astype(jnp.float32)
-        out_ref[2 * tile, :K, :] = jnp.where(low, real, turn(imag)).astype(jnp.bfloat16)
-        out_ref[2 * tile + 1, :K, :] = jnp.where(low, turn(real), imag).astype(jnp.bfloat16)
+        real = source_ref[0, :, lanes]
+        imag = source_ref[1, :, lanes]
+        out[2 * tile, :K, :] = jnp.concatenate([real[:, :HALF], imag[:, :HALF]], axis=1)
+        out[2 * tile + 1, :K, :] = jnp.concatenate([real[:, HALF:], imag[:, HALF:]], axis=1)
         frame = frame_ref[step * (tiles // 2) + tile // 2]
         velocity = velocity_ref[:, pl.ds((tile % 2) * LANES, LANES)]
-        product = jnp.broadcast_to((frame * velocity) & (VGRID - 1), (8, LANES))
+        product = (frame * velocity) & (VGRID - 1)
         high_part = (product >> 6).astype(jnp.float32)
         low_part = (product & 63).astype(jnp.float32)
-        even = jnp.where(small_low, high_part, turn(low_part))
-        odd = jnp.where(small_low, turn(high_part), low_part)
-        out_ref[2 * tile, K:, :] = jnp.where(own_row, even, width).astype(jnp.bfloat16)
-        out_ref[2 * tile + 1, K:, :] = jnp.where(own_row, odd, width).astype(jnp.bfloat16)
-
-
-def pack(info, window, frame_index, velocity_index, sources):
-    steps = 4
+        even = jnp.where(low, high_part, turn(low_part))
+        odd = jnp.where(low, turn(high_part), low_part)
+        out[2 * tile, K:, :] = jnp.concatenate([even, width], axis=0).astype(jnp.bfloat16)
+        out[2 * tile + 1, K:, :] = jnp.concatenate([odd, width], axis=0).astype(jnp.bfloat16)
+
+
+def pack(window, frame_index, velocity_index, sources):
+    steps = 2
     width = COLS // steps
     return pl.pallas_call(
         pack_kernel,
         grid=(steps,),
-        out_shape=jax.ShapeDtypeStruct((BOXES, ROWS, LANES), jnp.bfloat16),
+        out_shape=jax.ShapeDtypeStruct((BOXES, ROWS // 2, 2, LANES), jnp.bfloat16),
         in_specs=[
-            pl.BlockSpec(memory_space=pltpu.SMEM),
             pl.BlockSpec(memory_space=pltpu.SMEM),
             pl.BlockSpec(memory_space=pltpu.SMEM),
             pl.BlockSpec((1, 2 * LANES), lambda s: (0, 0)),
             pl.BlockSpec((2, K, width), lambda s: (0, 0, s)),
         ],
-        out_specs=pl.BlockSpec((BOXES // steps, ROWS, LANES), lambda s: (s, 0, 0)),
+        out_specs=pl.BlockSpec((BOXES // steps, ROWS // 2, 2, LANES), lambda s: (s, 0, 0, 0)),
         cost_estimate=pl.CostEstimate(flops=4 << 20, bytes_accessed=2 << 20, transcendentals=0),
         name="pack",
-    )(info, window, frame_index, velocity_index, sources)
+    )(window, frame_index, velocity_index, sources)
 
 
 def butterfly_kernel(
-    info_ref,
-    got_ref,
+    place_ref,
+    message_ref,
     mats_ref,
     eval_ref,
     picture_ref,
@@ -91,7 +89,7 @@
     cos_ref,
     sin_ref,
 ):
-    low = lane_low((K, LANES))
+    got_ref = message_ref.reshape(BOXES, ROWS, LANES)
     small_low = lane_low((8, LANES))
     row = lax.broadcasted_iota(jnp.int32, (8, LANES), 0)
     for pair in range(YBOX // 2):
@@ -103,8 +101,8 @@
             width = jnp.zeros((8, LANES), jnp.float32)
             for z in range(ZBOX):
                 extra = got_ref[z * YBOX + y, K:, :].astype(jnp.float32)
-                index = jnp.where(row == z, extra, index)
-                width = jnp.where(row == (z + 1) % ZBOX, extra, width)
+                index = jnp.where(row == z, extra[:1], index)
+                width = jnp.where(row == z, extra[1:], width)
             indices.append(index)
             widths.append(width)
         high_part = jnp.where(small_low, indices[0], turn(indices[1]))
@@ -125,10 +123,10 @@
     for z in range(ZBOX):
         for pair in range(YBOX // 2):
             lanes = pl.ds(pair * LANES, LANES)
-            even = got_ref[z * YBOX + 2 * pair, :K, :].astype(jnp.float32)
-            odd = got_ref[z * YBOX + 2 * pair + 1, :K, :].astype(jnp.float32)
-            state_ref[z, :K, lanes] = jnp.where(low, even, turn(odd)).astype(jnp.bfloat16)
-            state_ref[z, K:, lanes] = jnp.where(low, turn(even), odd).astype(jnp.bfloat16)
+            even = got_ref[z * YBOX + 2 * pair, :K, :]
+            odd = got_ref[z * YBOX + 2 * pair + 1, :K, :]
+            state_ref[z, :K, lanes] = jnp.concatenate([even[:, :HALF], odd[:, :HALF]], axis=1)
+            state_ref[z, K:, lanes] = jnp.concatenate([even[:, HALF:], odd[:, HALF:]], axis=1)
 
     def rotated(level, z, lanes, total):
         cosine = cos_ref[level, pl.ds(z, 1), lanes]
@@ -157,8 +155,8 @@
         picture_ref[z] = jnp.dot(
             eval_ref[...], state_ref[z], preferred_element_type=jnp.float32
         ).astype(jnp.bfloat16)
-    last = info_ref[1] == 7
-    first = info_ref[1] == 0
+    last = place_ref[0] == 7
+    first = place_ref[0] == 0
     nothing = jnp.zeros((16, WIDE), jnp.bfloat16)
     for z in range(ZBOX):
 
@@ -179,7 +177,7 @@
             above_ref[z] = picture_ref[z, :16, :]
 
 
-def butterfly(info, got, mats, evaluate):
+def butterfly(place, got, mats, evaluate):
     whole = pl.BlockSpec(memory_space=pltpu.VMEM)
     return pl.pallas_call(
         butterfly_kernel,
@@ -197,8 +195,9 @@
             pltpu.VMEM((LEVELS, ZBOX, WIDE), jnp.float32),
         ],
         cost_estimate=pl.CostEstimate(flops=2 << 30, bytes_accessed=3 << 20, transcendentals=8192),
+        compiler_params=pltpu.CompilerParams(vmem_limit_bytes=12 << 20),
         name="butterfly",
-    )(info, got, mats, evaluate)
+    )(place, got, mats, evaluate)
 
 
 def smooth_kernel(picture_ref, below_ref, above_ref, width_ref, sums_ref, out_ref):
@@ -223,7 +222,7 @@
             beside = turn(jnp.where(upper, left, right))
             field = jnp.concatenate([here, beside], axis=0).astype(jnp.bfloat16)
             sums = jnp.dot(sums_ref[...], field, preferred_element_type=jnp.float32)
-            wide = width_ref[pl.ds((z + 1) % ZBOX, 1), pl.ds(pair * LANES, LANES)] > 1.5
+            wide = width_ref[pl.ds(z, 1), pl.ds(pair * LANES, LANES)] > 1.5
             chosen = jnp.where(wide, sums[K:] / 25.0, sums[:K] / 9.0)
             top, bottom = chosen[:32], chosen[32:]
             box = z * YBOX + 2 * pair
@@ -240,18 +239,18 @@
         in_specs=[whole] * 5,
         out_specs=whole,
         cost_estimate=pl.CostEstimate(flops=1 << 28, bytes_accessed=2 << 20, transcendentals=0),
+        compiler_params=pltpu.CompilerParams(vmem_limit_bytes=12 << 20),
         name="smooth",
     )(picture, below, above, widths, sums)
 
 
 def unpack_kernel(got_ref, out_ref):
-    low = lane_low((32, LANES))
     for tile in range(out_ref.shape[-1] // LANES):
         lanes = pl.ds(tile * LANES, LANES)
-        even = got_ref[2 * tile].astype(jnp.float32)
-        odd = got_ref[2 * tile + 1].astype(jnp.float32)
-        out_ref[:32, lanes] = jnp.where(low, even, turn(odd)).astype(jnp.bfloat16)
-        out_ref[32:, lanes] = jnp.where(low, turn(even), odd).astype(jnp.bfloat16)
+        even = got_ref[2 * tile]
+        odd = got_ref[2 * tile + 1]
+        out_ref[:32, lanes] = jnp.concatenate([even[:, :HALF], odd[:, :HALF]], axis=1)
+        out_ref[32:, lanes] = jnp.concatenate([even[:, HALF:], odd[:, HALF:]], axis=1)
 
 
 def unpack(got):
@@ -263,6 +262,7 @@
         in_specs=[pl.BlockSpec((BOXES // steps, 32, LANES), lambda s: (s, 0, 0))],
         out_specs=pl.BlockSpec((K, COLS // steps), lambda s: (0, s)),
         cost_estimate=pl.CostEstimate(flops=1 << 20, bytes_accessed=1 << 20, transcendentals=0),
+        compiler_params=pltpu.CompilerParams(vmem_limit_bytes=12 << 20),
         name="unpack",
     )(got)
 
@@ -291,11 +291,8 @@
 def on_device(
     sources, translate_re, translate_im, frame_index, velocity_index, eval_re, eval_im, window
 ):
-    z = lax.axis_index("zh") * 2 + lax.axis_index("zl")
-    place = lax.broadcasted_iota(jnp.int32, (2,), 0)
-    info = jnp.where(place == 0, z, lax.axis_index("xc"))
     message = pack(
-        info, window.reshape(1), frame_index.reshape(16), velocity_index.reshape(1, 256), sources[0, 0]
+        window.reshape(1), frame_index.reshape(16), velocity_index.reshape(1, 256), sources[0, 0]
     )
     got = lax.all_to_all(message, GROUP, 0, 0, tiled=True)
     own = blocks(translate_re[:, :, 0], translate_im[:, :, 0])
@@ -308,7 +305,7 @@
         axis=-2,
     )
     evaluate = jnp.concatenate([eval_re, -eval_im], axis=1)
-    picture, last_rows, first_rows, widths = butterfly(info, got, mats, evaluate)
+    picture, last_rows, first_rows, widths = butterfly(lax.axis_index("xc").reshape(1), got, mats, evaluate)
     below = lax.ppermute(last_rows, "xc", [(i, (i + 1) % 8) for i in range(8)])
     above = lax.ppermute(first_rows, "xc", [(i, (i + 7) % 8) for i in range(8)])
     smoothed = smooth(picture, below, above, widths, jnp.asarray(box_sums(), jnp.bfloat16))

time: 97.7 us -> 86.8 us (0.89)
  Pallas kernels: 12.9 us -> 7.01 us
  other arithmetic: 2.37 us -> 0.49 us
  local copies, waits for them, and re-layouts: 1.89 us -> 0.14 us
    pallas_call x1, Pallas kernels: 4.49 us -> 2.4 us  [butterfly(): pl.pallas_call(butterfly_kernel, out_shape=(jax.ShapeDtypeStruct((ZBOX, K...]
    pallas_call x1, Pallas kernels: 2.82 us -> 0.9 us  [smooth(): pl.pallas_call(smooth_kernel, out_shape=jax.ShapeDtypeStruct((BOXES, 32,...]
    unnamed x14 -> x10, local copies, waits for them, and re-layouts: 1.78 us -> 0.02 us
  transfers between devices with their start and end apart: 3 -> 3, of which waited for: 2 -> 2; matrix products, arithmetic and copies ran while one was open for 2% -> 1% of each run, Pallas kernels for 0% -> 0%
where the time goes in v2:
time: 86.8 us; the launch traced here: 86.5 us
  waiting for transfers between devices  31.9 us (37%)
  blocking collectives  26.5 us (31%)
  starting transfers between devices  19.7 us (23%)
  Pallas kernels  7.01 us (8%)
    all_to_all x1, waiting for transfers between devices, on_device(): got = lax.all_to_all(message, GROUP, 0, 0, tiled=True)  29.3 us
    all_to_all x1, blocking collectives, on_device(): back = lax.all_to_all(smoothed, GROUP, 0, 0, tiled=True)  26.5 us
    all_to_all x1, starting transfers between devices, on_device(): got = lax.all_to_all(message, GROUP, 0, 0, tiled=True)  16.7 us
    ppermute x1, starting transfers between devices, on_device(): above = lax.ppermute(first_rows, 'xc', [(i, (i + 7) % 8) for i in range(8)])  2.94 us
    pallas_call x1, Pallas kernels, pack(): pl.pallas_call(pack_kernel, grid=(steps,), out_shape=jax.ShapeDtypeStruct...  2.72 us
    ppermute x1, waiting for transfers between devices, on_device(): below = lax.ppermute(last_rows, 'xc', [(i, (i + 1) % 8) for i in range(8)])  2.65 us
    pallas_call x1, Pallas kernels, butterfly(): pl.pallas_call(butterfly_kernel, out_shape=(jax.ShapeDtypeStruct((ZBOX, K...  2.4 us
  transfers between devices with their start and end apart: 3, of which 2 were waited for; matrix products, arithmetic and copies ran while one was open for 1% of the time, Pallas kernels for 0%

profile of v2, /device:TPU:8, one launch (start us, length us, event | category | flops | bytes accessed | tf_op | source)
XLA Modules:
  0.0 86.5 jit_solution(9472223673695181565)
XLA Ops:
  0.7 2.7 %pack.1 = bf16[64,33,2,128]{3,2,1,0:T(2,128)(2,1)} custom-call(s32[1]{0:T(128)} %bitcast.26.window_ref, s32[16]{0:T(128)} %bitcast.29, s32[1,256]{1,0:T(1,128)} %bitcast.28, bf16[2,64,4096]{2,1,0:T(8,128)(2,1)} %bitcast.27), custom_call_target="tpu_custom_call" | custom-call | flops 4194304 | bytes 2097152 | tf_op jit(solution)/shard_map/pack/pallas_call | solution.py:63
  3.4 0.0 copy-start.4
  3.4 0.0 copy-start.3
  3.4 0.0 copy-start.1
  3.4 0.0 copy-start.2
  3.4 16.7 %all-to-all-start = ((bf16[64,33,2,128]{3,2,1,0:T(2,128)(2,1)}), bf16[64,33,2,128]{3,2,1,0:T(2,128)(2,1)S(1)}, u32[]{:S(2)}, u32[]{:S(2)}) async-start(bf16[64,33,2,128]{3,2,1,0:T(2,128)(2,1)} %pack.1), calls=%async_computation | async-start | bytes 2162688 | tf_op jit(solution)/shard_map/all_to_all | solution.py:297
  20.1 0.0 copy-done.4
  20.2 0.0 copy-done.3
  20.2 0.1 pad_maximum_fusion.eval_ref
  20.2 0.0 copy-done.1
  20.3 0.0 copy-done.2
  20.4 0.2 maximum_maximum_fusion.1
  20.6 0.2 maximum_maximum_fusion.2
  20.8 0.1 maximum_maximum_fusion.mats_ref
  20.9 29.3 %all-to-all-done.message_ref = bf16[64,33,2,128]{3,2,1,0:T(2,128)(2,1)S(1)} async-done(((bf16[64,33,2,128]{3,2,1,0:T(2,128)(2,1)}), bf16[64,33,2,128]{3,2,1,0:T(2,128)(2,1)S(1)}, u32[]{:S(2)}, u32[]{:S(2)}) %all-to-all-start) | async-done | bytes 1081376 | tf_op jit(solution)/shard_map/all_to_all | solution.py:297
  50.1 0.0 copy-start
  50.1 2.4 %butterfly.1 = (bf16[8,64,512]{2,1,0:T(8,128)(2,1)S(1)}, bf16[8,16,512]{2,1,0:T(8,128)(2,1)S(1)}, bf16[8,16,512]{2,1,0:T(8,128)(2,1)S(1)}, f32[8,512]{1,0:T(8,128)S(1)}) custom-call(s32[1]{0:T(128)} %bitcast.place_ref, bf16[64,33,2,128]{3,2,1,0:T(2,128)(2,1)S(1)} %all-to-all-done.message_ref, bf16[4,256,256]{2,1,0:T(8,128)(2,1)S(1)} %maximum_maximum_fusion.mats_ref, ...), custom_call_target="tpu_custom_call" | custom-call | flops 2147483648 | bytes 3145728 | tf_op jit(solution)/shard_map/butterfly/pallas_call | solution.py:182
  52.5 0.0 collective-permute-start
  52.6 2.9 %collective-permute-start.1 = (bf16[8,16,512]{2,1,0:T(8,128)(2,1)S(1)}, bf16[8,16,512]{2,1,0:T(8,128)(2,1)S(1)}, u32[]{:S(2)}, u32[]{:S(2)}) collective-permute-start(bf16[8,16,512]{2,1,0:T(8,128)(2,1)S(1)} %get-tuple-element.11), channel_id=1, source_target_pairs={{0,112},{16,0},{32,16},{48,32},{64,48},{80,64},{96,80},{112,96},{1... | collective-permute-start | bytes 393224 | tf_op jit(solution)/shard_map/ppermute | solution.py:310
  55.5 2.6 %collective-permute-done.below_ref = bf16[8,16,512]{2,1,0:T(8,128)(2,1)S(1)} collective-permute-done((bf16[8,16,512]{2,1,0:T(8,128)(2,1)S(1)}, bf16[8,16,512]{2,1,0:T(8,128)(2,1)S(1)}, u32[]{:S(2)}, u32[]{:S(2)}) %collective-permute-start) | collective-permute-done | bytes 131104 | tf_op jit(solution)/shard_map/ppermute | solution.py:309
  58.2 0.0 collective-permute-done.1.above_ref
  58.2 0.0 copy-done
  58.2 0.9 %smooth.1 = bf16[64,32,128]{2,1,0:T(8,128)(2,1)S(1)} custom-call(bf16[8,64,512]{2,1,0:T(8,128)(2,1)S(1)} %get-tuple-element.9.picture_ref, bf16[8,16,512]{2,1,0:T(8,128)(2,1)S(1)} %collective-permute-done.below_ref, bf16[8,16,512]{2,1,0:T(8,128)(2,1)S(1)} %collective-permute-done.1.above_ref, f32[8,512]{1,0:T(8,128)S(1)} %get-tuple-element.12.width_ref, ...), custom_call_target="tpu_custom_call" | custom-call | flops 268435456 | bytes 2097152 | tf_op jit(solution)/shard_map/smooth/pallas_call | solution.py:236
  59.1 26.5 %all_to_all.10.got_ref = bf16[64,32,128]{2,1,0:T(8,128)(2,1)S(1)} all-to-all(bf16[64,32,128]{2,1,0:T(8,128)(2,1)S(1)} %smooth.1), channel_id=1, replica_groups=mesh['zh'=4,'xc'=8,'zl'=2,'y'=8] {'zh','zl','y'}, dimensions={0} | all-to-all | bytes 1048576 | tf_op jit(solution)/shard_map/all_to_all | solution.py:312
  85.5 1.0 %unpack.1 = bf16[64,4096]{1,0:T(8,128)(2,1)} custom-call(bf16[64,32,128]{2,1,0:T(8,128)(2,1)S(1)} %all_to_all.10.got_ref), custom_call_target="tpu_custom_call" | custom-call | flops 1048576 | bytes 1048576 | tf_op jit(solution)/shard_map/unpack/pallas_call | solution.py:258
  (8 shorter events, 0.2 us)
Async XLA Ops:
  3.4 16.8 %copy-start.4 = (bf16[64,64]{1,0:T(8,128)(2,1)S(1)}, bf16[64,64]{1,0:T(8,128)(2,1)}, u32[]{:S(2)}) copy-start(bf16[64,64]{1,0:T(8,128)(2,1)} %param.15) | copy-start | bytes 24580
  3.4 16.8 %copy-start.3 = (bf16[64,64]{1,0:T(8,128)(2,1)S(1)}, bf16[64,64]{1,0:T(8,128)(2,1)}, u32[]{:S(2)}) copy-start(bf16[64,64]{1,0:T(8,128)(2,1)} %param.14) | copy-start | bytes 24580
  3.4 16.9 %copy-start.1 = (bf16[4,2,2,64,64]{4,3,2,1,0:T(8,128)(2,1)S(1)}, bf16[4,2,2,64,64]{4,3,2,1,0:T(8,128)(2,1)}, u32[]{:S(2)}) copy-start(bf16[4,2,2,64,64]{4,3,2,1,0:T(8,128)(2,1)} %param.10) | copy-start | bytes 393220
  3.4 16.9 %copy-start.2 = (bf16[4,2,2,64,64]{4,3,2,1,0:T(8,128)(2,1)S(1)}, bf16[4,2,2,64,64]{4,3,2,1,0:T(8,128)(2,1)}, u32[]{:S(2)}) copy-start(bf16[4,2,2,64,64]{4,3,2,1,0:T(8,128)(2,1)} %param.11) | copy-start | bytes 393220
  3.4 46.7 %all-to-all-start = ((bf16[64,33,2,128]{3,2,1,0:T(2,128)(2,1)}), bf16[64,33,2,128]{3,2,1,0:T(2,128)(2,1)S(1)}, u32[]{:S(2)}, u32[]{:S(2)}) async-start(bf16[64,33,2,128]{3,2,1,0:T(2,128)(2,1)} %pack.1), calls=%async_computation | async-start | bytes 2162688 | tf_op jit(solution)/shard_map/all_to_all | solution.py:297
  50.1 8.0 %copy-start = (bf16[128,192]{1,0:T(8,128)(2,1)S(1)}, bf16[128,192]{1,0:T(8,128)(2,1)}, u32[]{:S(2)}) copy-start(bf16[128,192]{1,0:T(8,128)(2,1)} %constant.8.clone.sums_ref) | copy-start | bytes 147460
  52.5 5.6 %collective-permute-start = (bf16[8,16,512]{2,1,0:T(8,128)(2,1)S(1)}, bf16[8,16,512]{2,1,0:T(8,128)(2,1)S(1)}, u32[]{:S(2)}, u32[]{:S(2)}) collective-permute-start(bf16[8,16,512]{2,1,0:T(8,128)(2,1)S(1)} %get-tuple-element.10), channel_id=1, source_target_pairs={{0,16},{16,32},{32,48},{48,64},{64,80},{80,96},{96,112},{112,0},{1... | collective-permute-start | bytes 393224 | tf_op jit(solution)/shard_map/ppermute | solution.py:309
  52.6 5.6 %collective-permute-start.1 = (bf16[8,16,512]{2,1,0:T(8,128)(2,1)S(1)}, bf16[8,16,512]{2,1,0:T(8,128)(2,1)S(1)}, u32[]{:S(2)}, u32[]{:S(2)}) collective-permute-start(bf16[8,16,512]{2,1,0:T(8,128)(2,1)S(1)} %get-tuple-element.11), channel_id=1, source_target_pairs={{0,112},{16,0},{32,16},{48,32},{64,48},{80,64},{96,80},{112,96},{1... | collective-permute-start | bytes 393224 | tf_op jit(solution)/shard_map/ppermute | solution.py:310

commit v3 on v2

--- a/solution.py
+++ b/solution.py
@@ -82,8 +82,8 @@
     mats_ref,
     eval_ref,
     picture_ref,
-    below_ref,
-    above_ref,
+    inner_ref,
+    outer_ref,
     width_ref,
     state_ref,
     cos_ref,
@@ -155,26 +155,23 @@
         picture_ref[z] = jnp.dot(
             eval_ref[...], state_ref[z], preferred_element_type=jnp.float32
         ).astype(jnp.bfloat16)
-    last = place_ref[0] == 7
-    first = place_ref[0] == 0
-    nothing = jnp.zeros((16, WIDE), jnp.bfloat16)
+    place = place_ref[0]
+    even = place % 2 == 0
     for z in range(ZBOX):
-
-        @pl.when(last)
+        first_rows, last_rows = picture_ref[z, :16, :], picture_ref[z, 48:, :]
+        nothing = jnp.zeros_like(first_rows)
+        next_rows = picture_ref[z + 2, :16, :] if z + 2 < ZBOX else nothing
+        previous_rows = picture_ref[z - 2, 48:, :] if z >= 2 else nothing
+
+        @pl.when(even)
         def _():
-            below_ref[z] = picture_ref[z - 2, 48:, :] if z >= 2 else nothing
-
-        @pl.when(jnp.logical_not(last))
+            inner_ref[z] = last_rows
+            outer_ref[z] = jnp.where(place == 0, next_rows, first_rows)
+
+        @pl.when(jnp.logical_not(even))
         def _():
-            below_ref[z] = picture_ref[z, 48:, :]
-
-        @pl.when(first)
-        def _():
-            above_ref[z] = picture_ref[z + 2, :16, :] if z + 2 < ZBOX else nothing
-
-        @pl.when(jnp.logical_not(first))
-        def _():
-            above_ref[z] = picture_ref[z, :16, :]
+            inner_ref[z] = first_rows
+            outer_ref[z] = jnp.where(place == 7, previous_rows, last_rows)
 
 
 def butterfly(place, got, mats, evaluate):
@@ -200,8 +197,9 @@
     )(place, got, mats, evaluate)
 
 
-def smooth_kernel(picture_ref, below_ref, above_ref, width_ref, sums_ref, out_ref):
+def smooth_kernel(place_ref, picture_ref, inner_ref, outer_ref, width_ref, sums_ref, out_ref):
     rows = K + 32
+    even = place_ref[0] % 2 == 0
     low = lane_low((rows, LANES))
     half_low = lane_low((32, LANES))
     upper = lax.broadcasted_iota(jnp.int32, (rows, LANES), 0) % 8 >= 4
@@ -209,7 +207,9 @@
 
     def tile(z, pair):
         lanes = pl.ds(pair * LANES, LANES)
-        parts = [below_ref[z, :, lanes], picture_ref[z, :, lanes], above_ref[z, :, lanes]]
+        inner, outer = inner_ref[z, :, lanes], outer_ref[z, :, lanes]
+        below, above = jnp.where(even, outer, inner), jnp.where(even, inner, outer)
+        parts = [below, picture_ref[z, :, lanes], above]
         return jnp.concatenate(parts, axis=0).astype(jnp.float32)
 
     for zh in range(ZBOX // 2):
@@ -231,17 +231,17 @@
             before, here = here, after
 
 
-def smooth(picture, below, above, widths, sums):
+def smooth(place, picture, inner, outer, widths, sums):
     whole = pl.BlockSpec(memory_space=pltpu.VMEM)
     return pl.pallas_call(
         smooth_kernel,
         out_shape=jax.ShapeDtypeStruct((BOXES, 32, LANES), jnp.bfloat16),
-        in_specs=[whole] * 5,
+        in_specs=[pl.BlockSpec(memory_space=pltpu.SMEM)] + [whole] * 5,
         out_specs=whole,
         cost_estimate=pl.CostEstimate(flops=1 << 28, bytes_accessed=2 << 20, transcendentals=0),
         compiler_params=pltpu.CompilerParams(vmem_limit_bytes=12 << 20),
         name="smooth",
-    )(picture, below, above, widths, sums)
+    )(place, picture, inner, outer, widths, sums)
 
 
 def unpack_kernel(got_ref, out_ref):
@@ -305,10 +305,12 @@
         axis=-2,
     )
     evaluate = jnp.concatenate([eval_re, -eval_im], axis=1)
-    picture, last_rows, first_rows, widths = butterfly(lax.axis_index("xc").reshape(1), got, mats, evaluate)
-    below = lax.ppermute(last_rows, "xc", [(i, (i + 1) % 8) for i in range(8)])
-    above = lax.ppermute(first_rows, "xc", [(i, (i + 7) % 8) for i in range(8)])
-    smoothed = smooth(picture, below, above, widths, jnp.asarray(box_sums(), jnp.bfloat16))
+    place = lax.axis_index("xc").reshape(1)
+    picture, inner, outer, widths = butterfly(place, got, mats, evaluate)
+    inner = lax.ppermute(inner, "xc", [(i, i ^ 1) for i in range(8)])
+    outer = lax.ppermute(outer, "xc", [(i, (i + 1 if i % 2 else i + 7) % 8) for i in range(8)])
+    sums = jnp.asarray(box_sums(), jnp.bfloat16)
+    smoothed = smooth(place, picture, inner, outer, widths, sums)
     back = lax.all_to_all(smoothed, GROUP, 0, 0, tiled=True)
     return unpack(back).reshape(TILE, TILE, COLS)
 

time: 86.8 us -> 90.3 us (1.040)
  the two profiles are of different devices: /device:TPU:8 before, /device:TPU:15 now
where the time goes in v3:
time: 90.3 us; the launch traced here: 90 us
  waiting for transfers between devices  33.6 us (37%)
  blocking collectives  25.5 us (28%)
  starting transfers between devices  22.5 us (25%)
  Pallas kernels  6.98 us (8%)
    all_to_all x1, waiting for transfers between devices, on_device(): got = lax.all_to_all(message, GROUP, 0, 0, tiled=True)  28.1 us
    all_to_all x1, blocking collectives, on_device(): back = lax.all_to_all(smoothed, GROUP, 0, 0, tiled=True)  25.5 us
    all_to_all x1, starting transfers between devices, on_device(): got = lax.all_to_all(message, GROUP, 0, 0, tiled=True)  16.2 us
    ppermute x1, waiting for transfers between devices, on_device(): lax.ppermute(outer, 'xc', [(i, (i + 1 if i % 2 else i + 7) % 8) for i in...  5.47 us
    ppermute x1, starting transfers between devices, on_device(): inner = lax.ppermute(inner, 'xc', [(i, i ^ 1) for i in range(8)])  4.35 us
    pallas_call x1, Pallas kernels, pack(): pl.pallas_call(pack_kernel, grid=(steps,), out_shape=jax.ShapeDtypeStruct...  2.72 us
    pallas_call x1, Pallas kernels, butterfly(): pl.pallas_call(butterfly_kernel, out_shape=(jax.ShapeDtypeStruct((ZBOX, K...  2.38 us
    ppermute x1, starting transfers between devices, on_device(): lax.ppermute(outer, 'xc', [(i, (i + 1 if i % 2 else i + 7) % 8) for i in...  2.01 us
  transfers between devices with their start and end apart: 3, of which 2 were waited for; matrix products, arithmetic and copies ran while one was open for 1% of the time, Pallas kernels for 0%

profile of v3, /device:TPU:15, one launch (start us, length us, event | category | flops | bytes accessed | tf_op | source)
XLA Modules:
  0.0 90.0 jit_solution(3541014769759210365)
XLA Ops:
  0.7 2.7 %pack.1 = bf16[64,33,2,128]{3,2,1,0:T(2,128)(2,1)} custom-call(s32[1]{0:T(128)} %bitcast.26.window_ref, s32[16]{0:T(128)} %bitcast.29, s32[1,256]{1,0:T(1,128)} %bitcast.28, bf16[2,64,4096]{2,1,0:T(8,128)(2,1)} %bitcast.27), custom_call_target="tpu_custom_call" | custom-call | flops 4194304 | bytes 2097152 | tf_op jit(solution)/shard_map/pack/pallas_call | solution.py:63
  3.4 0.0 copy-start.4
  3.4 0.0 copy-start.3
  3.4 0.0 copy-start.1
  3.4 0.0 copy-start.2
  3.4 16.2 %all-to-all-start = ((bf16[64,33,2,128]{3,2,1,0:T(2,128)(2,1)}), bf16[64,33,2,128]{3,2,1,0:T(2,128)(2,1)S(1)}, u32[]{:S(2)}, u32[]{:S(2)}) async-start(bf16[64,33,2,128]{3,2,1,0:T(2,128)(2,1)} %pack.1), calls=%async_computation | async-start | bytes 2162688 | tf_op jit(solution)/shard_map/all_to_all | solution.py:297
  19.6 0.0 copy-done.4
  19.6 0.0 copy-done.3
  19.6 0.1 pad_maximum_fusion.eval_ref
  19.7 0.0 copy-done.1
  19.7 0.0 copy-done.2
  19.9 0.2 maximum_maximum_fusion.1
  20.0 0.2 maximum_maximum_fusion.2
  20.2 0.1 maximum_maximum_fusion.mats_ref
  20.3 28.1 %all-to-all-done.message_ref = bf16[64,33,2,128]{3,2,1,0:T(2,128)(2,1)S(1)} async-done(((bf16[64,33,2,128]{3,2,1,0:T(2,128)(2,1)}), bf16[64,33,2,128]{3,2,1,0:T(2,128)(2,1)S(1)}, u32[]{:S(2)}, u32[]{:S(2)}) %all-to-all-start) | async-done | bytes 1081376 | tf_op jit(solution)/shard_map/all_to_all | solution.py:297
  48.4 0.0 copy-start
  48.4 2.4 %butterfly.1 = (bf16[8,64,512]{2,1,0:T(8,128)(2,1)S(1)}, bf16[8,16,512]{2,1,0:T(8,128)(2,1)S(1)}, bf16[8,16,512]{2,1,0:T(8,128)(2,1)S(1)}, f32[8,512]{1,0:T(8,128)S(1)}) custom-call(s32[1]{0:T(128)} %bitcast.place_ref, bf16[64,33,2,128]{3,2,1,0:T(2,128)(2,1)S(1)} %all-to-all-done.message_ref, bf16[4,256,256]{2,1,0:T(8,128)(2,1)S(1)} %maximum_maximum_fusion.mats_ref, ...), custom_call_target="tpu_custom_call" | custom-call | flops 2147483648 | bytes 3145728 | tf_op jit(solution)/shard_map/butterfly/pallas_call | solution.py:179
  50.8 4.3 %collective-permute-start = (bf16[8,16,512]{2,1,0:T(8,128)(2,1)S(1)}, bf16[8,16,512]{2,1,0:T(8,128)(2,1)S(1)}, u32[]{:S(2)}, u32[]{:S(2)}) collective-permute-start(bf16[8,16,512]{2,1,0:T(8,128)(2,1)S(1)} %get-tuple-element.10), channel_id=1, source_target_pairs={{0,16},{16,0},{32,48},{48,32},{64,80},{80,64},{96,112},{112,96},{1... | collective-permute-start | bytes 393224 | tf_op jit(solution)/shard_map/ppermute | solution.py:310
  55.1 2.0 %collective-permute-start.1 = (bf16[8,16,512]{2,1,0:T(8,128)(2,1)S(1)}, bf16[8,16,512]{2,1,0:T(8,128)(2,1)S(1)}, u32[]{:S(2)}, u32[]{:S(2)}) collective-permute-start(bf16[8,16,512]{2,1,0:T(8,128)(2,1)S(1)} %get-tuple-element.11), channel_id=1, source_target_pairs={{0,112},{16,32},{32,16},{48,64},{64,48},{80,96},{96,80},{112,0},{1... | collective-permute-start | bytes 393224 | tf_op jit(solution)/shard_map/ppermute | solution.py:311
  57.1 0.0 collective-permute-done.inner_ref
  57.1 5.5 %collective-permute-done.1.outer_ref = bf16[8,16,512]{2,1,0:T(8,128)(2,1)S(1)} collective-permute-done((bf16[8,16,512]{2,1,0:T(8,128)(2,1)S(1)}, bf16[8,16,512]{2,1,0:T(8,128)(2,1)S(1)}, u32[]{:S(2)}, u32[]{:S(2)}) %collective-permute-start.1) | collective-permute-done | bytes 131104 | tf_op jit(solution)/shard_map/ppermute | solution.py:311
  62.6 0.0 copy-done
  62.6 0.9 %smooth.1 = bf16[64,32,128]{2,1,0:T(8,128)(2,1)S(1)} custom-call(s32[1]{0:T(128)} %bitcast.place_ref, bf16[8,64,512]{2,1,0:T(8,128)(2,1)S(1)} %get-tuple-element.9.picture_ref, bf16[8,16,512]{2,1,0:T(8,128)(2,1)S(1)} %collective-permute-done.inner_ref, bf16[8,16,512]{2,1,0:T(8,128)(2,1)S(1)} %collective-permute-done.1.outer_ref, ...), custom_call_target="tpu_custom_call" | custom-call | flops 268435456 | bytes 2097152 | tf_op jit(solution)/shard_map/smooth/pallas_call | solution.py:236
  63.5 25.5 %all_to_all.10.got_ref = bf16[64,32,128]{2,1,0:T(8,128)(2,1)S(1)} all-to-all(bf16[64,32,128]{2,1,0:T(8,128)(2,1)S(1)} %smooth.1), channel_id=1, replica_groups=mesh['zh'=4,'xc'=8,'zl'=2,'y'=8] {'zh','zl','y'}, dimensions={0} | all-to-all | bytes 1048576 | tf_op jit(solution)/shard_map/all_to_all | solution.py:314
  89.0 1.0 %unpack.1 = bf16[64,4096]{1,0:T(8,128)(2,1)} custom-call(bf16[64,32,128]{2,1,0:T(8,128)(2,1)S(1)} %all_to_all.10.got_ref), custom_call_target="tpu_custom_call" | custom-call | flops 1048576 | bytes 1048576 | tf_op jit(solution)/shard_map/unpack/pallas_call | solution.py:258
  (8 shorter events, 0.2 us)
Async XLA Ops:
  3.4 16.2 %copy-start.4 = (bf16[64,64]{1,0:T(8,128)(2,1)S(1)}, bf16[64,64]{1,0:T(8,128)(2,1)}, u32[]{:S(2)}) copy-start(bf16[64,64]{1,0:T(8,128)(2,1)} %param.15) | copy-start | bytes 24580
  3.4 16.2 %copy-start.3 = (bf16[64,64]{1,0:T(8,128)(2,1)S(1)}, bf16[64,64]{1,0:T(8,128)(2,1)}, u32[]{:S(2)}) copy-start(bf16[64,64]{1,0:T(8,128)(2,1)} %param.14) | copy-start | bytes 24580
  3.4 16.3 %copy-start.1 = (bf16[4,2,2,64,64]{4,3,2,1,0:T(8,128)(2,1)S(1)}, bf16[4,2,2,64,64]{4,3,2,1,0:T(8,128)(2,1)}, u32[]{:S(2)}) copy-start(bf16[4,2,2,64,64]{4,3,2,1,0:T(8,128)(2,1)} %param.10) | copy-start | bytes 393220
  3.4 16.3 %copy-start.2 = (bf16[4,2,2,64,64]{4,3,2,1,0:T(8,128)(2,1)S(1)}, bf16[4,2,2,64,64]{4,3,2,1,0:T(8,128)(2,1)}, u32[]{:S(2)}) copy-start(bf16[4,2,2,64,64]{4,3,2,1,0:T(8,128)(2,1)} %param.11) | copy-start | bytes 393220
  3.4 45.0 %all-to-all-start = ((bf16[64,33,2,128]{3,2,1,0:T(2,128)(2,1)}), bf16[64,33,2,128]{3,2,1,0:T(2,128)(2,1)S(1)}, u32[]{:S(2)}, u32[]{:S(2)}) async-start(bf16[64,33,2,128]{3,2,1,0:T(2,128)(2,1)} %pack.1), calls=%async_computation | async-start | bytes 2162688 | tf_op jit(solution)/shard_map/all_to_all | solution.py:297
  48.4 14.2 %copy-start = (bf16[128,192]{1,0:T(8,128)(2,1)S(1)}, bf16[128,192]{1,0:T(8,128)(2,1)}, u32[]{:S(2)}) copy-start(bf16[128,192]{1,0:T(8,128)(2,1)} %constant.8.clone.sums_ref) | copy-start | bytes 147460
  50.8 6.4 %collective-permute-start = (bf16[8,16,512]{2,1,0:T(8,128)(2,1)S(1)}, bf16[8,16,512]{2,1,0:T(8,128)(2,1)S(1)}, u32[]{:S(2)}, u32[]{:S(2)}) collective-permute-start(bf16[8,16,512]{2,1,0:T(8,128)(2,1)S(1)} %get-tuple-element.10), channel_id=1, source_target_pairs={{0,16},{16,0},{32,48},{48,32},{64,80},{80,64},{96,112},{112,96},{1... | collective-permute-start | bytes 393224 | tf_op jit(solution)/shard_map/ppermute | solution.py:310
  55.1 7.5 %collective-permute-start.1 = (bf16[8,16,512]{2,1,0:T(8,128)(2,1)S(1)}, bf16[8,16,512]{2,1,0:T(8,128)(2,1)S(1)}, u32[]{:S(2)}, u32[]{:S(2)}) collective-permute-start(bf16[8,16,512]{2,1,0:T(8,128)(2,1)S(1)} %get-tuple-element.11), channel_id=1, source_target_pairs={{0,112},{16,32},{32,16},{48,64},{64,48},{80,96},{96,80},{112,0},{1... | collective-permute-start | bytes 393224 | tf_op jit(solution)/shard_map/ppermute | solution.py:311

commit v4 on v2

--- a/solution.py
+++ b/solution.py
@@ -58,7 +58,7 @@
 
 
 def pack(window, frame_index, velocity_index, sources):
-    steps = 2
+    steps = 1
     width = COLS // steps
     return pl.pallas_call(
         pack_kernel,

time: 86.8 us -> 87.1 us (level)
  no operation moved by 1% of the time
where the time goes in v4:
time: 87.1 us; the launch traced here: 86.8 us
  waiting for transfers between devices  31.9 us (37%)
  blocking collectives  26.5 us (30%)
  starting transfers between devices  19.7 us (23%)
  Pallas kernels  7.31 us (8%)
    all_to_all x1, waiting for transfers between devices, on_device(): got = lax.all_to_all(message, GROUP, 0, 0, tiled=True)  29.3 us
    all_to_all x1, blocking collectives, on_device(): back = lax.all_to_all(smoothed, GROUP, 0, 0, tiled=True)  26.5 us
    all_to_all x1, starting transfers between devices, on_device(): got = lax.all_to_all(message, GROUP, 0, 0, tiled=True)  16.7 us
    pallas_call x1, Pallas kernels, pack(): pl.pallas_call(pack_kernel, grid=(steps,), out_shape=jax.ShapeDtypeStruct...  3.02 us
    ppermute x1, starting transfers between devices, on_device(): above = lax.ppermute(first_rows, 'xc', [(i, (i + 7) % 8) for i in range(8)])  2.94 us
    ppermute x1, waiting for transfers between devices, on_device(): below = lax.ppermute(last_rows, 'xc', [(i, (i + 1) % 8) for i in range(8)])  2.65 us
    pallas_call x1, Pallas kernels, butterfly(): pl.pallas_call(butterfly_kernel, out_shape=(jax.ShapeDtypeStruct((ZBOX, K...  2.4 us
  transfers between devices with their start and end apart: 3, of which 2 were waited for; matrix products, arithmetic and copies ran while one was open for 1% of the time, Pallas kernels for 0%

profile of v4, /device:TPU:8, one launch (start us, length us, event | category | flops | bytes accessed | tf_op | source)
XLA Modules:
  0.0 86.8 jit_solution(7830826969696353510)
XLA Ops:
  0.7 3.0 %pack.1 = bf16[64,33,2,128]{3,2,1,0:T(2,128)(2,1)} custom-call(s32[1]{0:T(128)} %bitcast.26.window_ref, s32[16]{0:T(128)} %bitcast.29, s32[1,256]{1,0:T(1,128)} %bitcast.28, bf16[2,64,4096]{2,1,0:T(8,128)(2,1)} %bitcast.27), custom_call_target="tpu_custom_call" | custom-call | flops 4194304 | bytes 2097152 | tf_op jit(solution)/shard_map/pack/pallas_call | solution.py:63
  3.7 0.0 copy-start.4
  3.7 0.0 copy-start.3
  3.7 0.0 copy-start.1
  3.7 0.0 copy-start.2
  3.7 16.7 %all-to-all-start = ((bf16[64,33,2,128]{3,2,1,0:T(2,128)(2,1)}), bf16[64,33,2,128]{3,2,1,0:T(2,128)(2,1)S(1)}, u32[]{:S(2)}, u32[]{:S(2)}) async-start(bf16[64,33,2,128]{3,2,1,0:T(2,128)(2,1)} %pack.1), calls=%async_computation | async-start | bytes 2162688 | tf_op jit(solution)/shard_map/all_to_all | solution.py:297
  20.4 0.0 copy-done.4
  20.4 0.0 copy-done.3
  20.5 0.1 pad_maximum_fusion.eval_ref
  20.5 0.0 copy-done.1
  20.6 0.0 copy-done.2
  20.7 0.2 maximum_maximum_fusion.1
  20.9 0.2 maximum_maximum_fusion.2
  21.1 0.1 maximum_maximum_fusion.mats_ref
  21.1 29.3 %all-to-all-done.message_ref = bf16[64,33,2,128]{3,2,1,0:T(2,128)(2,1)S(1)} async-done(((bf16[64,33,2,128]{3,2,1,0:T(2,128)(2,1)}), bf16[64,33,2,128]{3,2,1,0:T(2,128)(2,1)S(1)}, u32[]{:S(2)}, u32[]{:S(2)}) %all-to-all-start) | async-done | bytes 1081376 | tf_op jit(solution)/shard_map/all_to_all | solution.py:297
  50.4 0.0 copy-start
  50.4 2.4 %butterfly.1 = (bf16[8,64,512]{2,1,0:T(8,128)(2,1)S(1)}, bf16[8,16,512]{2,1,0:T(8,128)(2,1)S(1)}, bf16[8,16,512]{2,1,0:T(8,128)(2,1)S(1)}, f32[8,512]{1,0:T(8,128)S(1)}) custom-call(s32[1]{0:T(128)} %bitcast.place_ref, bf16[64,33,2,128]{3,2,1,0:T(2,128)(2,1)S(1)} %all-to-all-done.message_ref, bf16[4,256,256]{2,1,0:T(8,128)(2,1)S(1)} %maximum_maximum_fusion.mats_ref, ...), custom_call_target="tpu_custom_call" | custom-call | flops 2147483648 | bytes 3145728 | tf_op jit(solution)/shard_map/butterfly/pallas_call | solution.py:182
  52.8 0.0 collective-permute-start
  52.9 2.9 %collective-permute-start.1 = (bf16[8,16,512]{2,1,0:T(8,128)(2,1)S(1)}, bf16[8,16,512]{2,1,0:T(8,128)(2,1)S(1)}, u32[]{:S(2)}, u32[]{:S(2)}) collective-permute-start(bf16[8,16,512]{2,1,0:T(8,128)(2,1)S(1)} %get-tuple-element.11), channel_id=1, source_target_pairs={{0,112},{16,0},{32,16},{48,32},{64,48},{80,64},{96,80},{112,96},{1... | collective-permute-start | bytes 393224 | tf_op jit(solution)/shard_map/ppermute | solution.py:310
  55.8 2.6 %collective-permute-done.below_ref = bf16[8,16,512]{2,1,0:T(8,128)(2,1)S(1)} collective-permute-done((bf16[8,16,512]{2,1,0:T(8,128)(2,1)S(1)}, bf16[8,16,512]{2,1,0:T(8,128)(2,1)S(1)}, u32[]{:S(2)}, u32[]{:S(2)}) %collective-permute-start) | collective-permute-done | bytes 131104 | tf_op jit(solution)/shard_map/ppermute | solution.py:309
  58.4 0.0 collective-permute-done.1.above_ref
  58.4 0.0 copy-done
  58.5 0.9 %smooth.1 = bf16[64,32,128]{2,1,0:T(8,128)(2,1)S(1)} custom-call(bf16[8,64,512]{2,1,0:T(8,128)(2,1)S(1)} %get-tuple-element.9.picture_ref, bf16[8,16,512]{2,1,0:T(8,128)(2,1)S(1)} %collective-permute-done.below_ref, bf16[8,16,512]{2,1,0:T(8,128)(2,1)S(1)} %collective-permute-done.1.above_ref, f32[8,512]{1,0:T(8,128)S(1)} %get-tuple-element.12.width_ref, ...), custom_call_target="tpu_custom_call" | custom-call | flops 268435456 | bytes 2097152 | tf_op jit(solution)/shard_map/smooth/pallas_call | solution.py:236
  59.4 26.5 %all_to_all.10.got_ref = bf16[64,32,128]{2,1,0:T(8,128)(2,1)S(1)} all-to-all(bf16[64,32,128]{2,1,0:T(8,128)(2,1)S(1)} %smooth.1), channel_id=1, replica_groups=mesh['zh'=4,'xc'=8,'zl'=2,'y'=8] {'zh','zl','y'}, dimensions={0} | all-to-all | bytes 1048576 | tf_op jit(solution)/shard_map/all_to_all | solution.py:312
  85.8 1.0 %unpack.1 = bf16[64,4096]{1,0:T(8,128)(2,1)} custom-call(bf16[64,32,128]{2,1,0:T(8,128)(2,1)S(1)} %all_to_all.10.got_ref), custom_call_target="tpu_custom_call" | custom-call | flops 1048576 | bytes 1048576 | tf_op jit(solution)/shard_map/unpack/pallas_call | solution.py:258
  (8 shorter events, 0.2 us)
Async XLA Ops:
  3.7 16.8 %copy-start.4 = (bf16[64,64]{1,0:T(8,128)(2,1)S(1)}, bf16[64,64]{1,0:T(8,128)(2,1)}, u32[]{:S(2)}) copy-start(bf16[64,64]{1,0:T(8,128)(2,1)} %param.15) | copy-start | bytes 24580
  3.7 16.8 %copy-start.3 = (bf16[64,64]{1,0:T(8,128)(2,1)S(1)}, bf16[64,64]{1,0:T(8,128)(2,1)}, u32[]{:S(2)}) copy-start(bf16[64,64]{1,0:T(8,128)(2,1)} %param.14) | copy-start | bytes 24580
  3.7 16.9 %copy-start.1 = (bf16[4,2,2,64,64]{4,3,2,1,0:T(8,128)(2,1)S(1)}, bf16[4,2,2,64,64]{4,3,2,1,0:T(8,128)(2,1)}, u32[]{:S(2)}) copy-start(bf16[4,2,2,64,64]{4,3,2,1,0:T(8,128)(2,1)} %param.10) | copy-start | bytes 393220
  3.7 16.9 %copy-start.2 = (bf16[4,2,2,64,64]{4,3,2,1,0:T(8,128)(2,1)S(1)}, bf16[4,2,2,64,64]{4,3,2,1,0:T(8,128)(2,1)}, u32[]{:S(2)}) copy-start(bf16[4,2,2,64,64]{4,3,2,1,0:T(8,128)(2,1)} %param.11) | copy-start | bytes 393220
  3.7 46.7 %all-to-all-start = ((bf16[64,33,2,128]{3,2,1,0:T(2,128)(2,1)}), bf16[64,33,2,128]{3,2,1,0:T(2,128)(2,1)S(1)}, u32[]{:S(2)}, u32[]{:S(2)}) async-start(bf16[64,33,2,128]{3,2,1,0:T(2,128)(2,1)} %pack.1), calls=%async_computation | async-start | bytes 2162688 | tf_op jit(solution)/shard_map/all_to_all | solution.py:297
  50.4 8.0 %copy-start = (bf16[128,192]{1,0:T(8,128)(2,1)S(1)}, bf16[128,192]{1,0:T(8,128)(2,1)}, u32[]{:S(2)}) copy-start(bf16[128,192]{1,0:T(8,128)(2,1)} %constant.8.clone.sums_ref) | copy-start | bytes 147460
  52.8 5.6 %collective-permute-start = (bf16[8,16,512]{2,1,0:T(8,128)(2,1)S(1)}, bf16[8,16,512]{2,1,0:T(8,128)(2,1)S(1)}, u32[]{:S(2)}, u32[]{:S(2)}) collective-permute-start(bf16[8,16,512]{2,1,0:T(8,128)(2,1)S(1)} %get-tuple-element.10), channel_id=1, source_target_pairs={{0,16},{16,32},{32,48},{48,64},{64,80},{80,96},{96,112},{112,0},{1... | collective-permute-start | bytes 393224 | tf_op jit(solution)/shard_map/ppermute | solution.py:309
  52.9 5.6 %collective-permute-start.1 = (bf16[8,16,512]{2,1,0:T(8,128)(2,1)S(1)}, bf16[8,16,512]{2,1,0:T(8,128)(2,1)S(1)}, u32[]{:S(2)}, u32[]{:S(2)}) collective-permute-start(bf16[8,16,512]{2,1,0:T(8,128)(2,1)S(1)} %get-tuple-element.11), channel_id=1, source_target_pairs={{0,112},{16,0},{32,16},{48,32},{64,48},{80,64},{96,80},{112,96},{1... | collective-permute-start | bytes 393224 | tf_op jit(solution)/shard_map/ppermute | solution.py:310
